TPU v7x, 32 devices: a whole 2x2x4 slice. The times are simulated.
32 devices in a mesh: term: 8 (over z, core), sector: 4 (over y, x).
Axes of the slice: x: 2, y: 2, z: 4, core: 2. Of those that a mesh axis runs over, the one named last changes fastest.
Arguments:
- wavefunction: bfloat16 [24, 256, 256], P('sector'), may hold values from -6 to 6
- left_env: bfloat16 [24, 24, 256, 256], P('term', 'sector')
- right_env: bfloat16 [24, 24, 256, 256], P('term', 'sector')
- source: int32 [24, 24], P('term'), may hold values from 0 to 23, as said below
- block_size: int32 [24, 2], P('sector'), may hold values from 32 to 256
Outputs:
- first_product: float32 [24, 256, 256], P('sector', 'term')
- second_product: float32 [24, 256, 256], P('sector', 'term')
Inputs may be any that keep to these rules, and one draw needn't show every extreme that they name: Owner of sector s is s // 6. Among the 3 x 6 entries of source in one device's rows (one index of term) and columns (one index of sector), at most 5 name sectors of any one owner, and some owner is named exactly 5 times.
All inputs are finite; a program needn't handle non-finite values.
Results may differ from a plain program's by a relative error of at most 0.0037.
Values may be sent and summed in bfloat16 or wider, within the bound.
A program may use at most 64 MiB of HBM per device.

v0:
```python
import jax
import jax.numpy as jnp
from jax import lax
from jax.sharding import PartitionSpec as P

epsilon = 1e-06


def block_mask(block_size, width):
    positions = jnp.arange(width, dtype=jnp.int32)
    row_keep = positions[None, :] < block_size[:, 0:1]
    column_keep = positions[None, :] < block_size[:, 1:2]
    return row_keep[:, :, None] & column_keep[:, None, :]


def fetch_blocks(masked, source):
    local_count = masked.shape[0]
    width = masked.shape[1]
    bond_count = source.shape[0]
    my_index = lax.axis_index("sector")
    item_count = bond_count * local_count
    wanted = lax.dynamic_slice_in_dim(source, my_index * local_count, local_count, 1).reshape(
        item_count
    )
    pieces = lax.all_gather(masked, "sector", axis=0, tiled=True)
    piece_count = pieces.shape[0]
    numbers = jnp.arange(piece_count, dtype=jnp.int32)
    onehot = (wanted[:, None] == numbers[None, :]).astype(jnp.bfloat16)
    picked = jnp.dot(
        onehot, pieces.reshape(piece_count, width * width), preferred_element_type=jnp.float32
    )
    return picked.astype(jnp.bfloat16).reshape(bond_count, local_count, width, width)


def apply_operator(vector, left_env, right_env, source, keep):
    masked = jnp.where(keep, vector, jnp.zeros_like(vector))
    picked = fetch_blocks(masked, source)
    half_product = jnp.einsum(
        "bkij,bkjl->bkil", left_env, picked, preferred_element_type=jnp.float32
    ).astype(jnp.bfloat16)
    bond_terms = jnp.einsum(
        "bkil,bkml->bkim", half_product, right_env, preferred_element_type=jnp.float32
    )
    summed = jnp.sum(bond_terms, axis=0)
    return (jnp.where(keep, summed, jnp.zeros_like(summed)), masked)


def body(wavefunction, left_env, right_env, source, block_size):
    width = wavefunction.shape[1]
    keep = block_mask(block_size, width)
    term_count = lax.axis_size("term")
    term_index = lax.axis_index("term")
    row_count = width // term_count
    total_count = lax.axis_size("sector") * wavefunction.shape[0] * width * width
    partial_value, masked = apply_operator(wavefunction, left_env, right_env, source, keep)
    masked_float = masked.astype(jnp.float32)
    whole_sum = lax.psum(partial_value, "term")
    first_product = lax.dynamic_slice_in_dim(whole_sum, term_index * row_count, row_count, 1)
    margin, self_norm = lax.psum(
        (jnp.sum(masked_float * whole_sum), jnp.sum(masked_float * masked_float)), "sector"
    )
    residual = whole_sum - margin / self_norm * masked_float
    spread = lax.psum(jnp.sum(residual * residual), "sector")
    next_vector = (residual * lax.rsqrt(spread / total_count + epsilon)).astype(jnp.bfloat16)
    second_partial, _ = apply_operator(next_vector, left_env, right_env, source, keep)
    second_product = lax.psum_scatter(second_partial, "term", scatter_dimension=1, tiled=True)
    return (first_product, second_product)


def solution(mesh):
    placed = (
        P("sector", None, None),
        P("term", "sector", None, None),
        P("term", "sector", None, None),
        P("term", None),
        P("sector", None),
    )
    return jax.shard_map(
        body,
        mesh=mesh,
        in_specs=placed,
        out_specs=(P("sector", "term", None), P("sector", "term", None)),
        check_vma=False,
    )
```

profile of v0, /device:TPU:0, one launch (start us, length us, event | category | flops | bytes accessed | tf_op | source)
XLA Modules:
  0.0 256.0 jit_solution(13237176541998194756)
XLA Ops:
  7.2 0.0 copy-start
  7.2 0.0 copy-start.2
  7.2 0.0 all-gather.3.cloned.1.call-start
  7.2 0.9 slice_bitcast_fusion.1
  8.1 0.1 iota_compare_fusion.3
  8.2 2.3 and_select_fusion.3
  10.5 0.0 all-gather.3.cloned.1.call-update
  10.5 0.0 all-reduce.3.cloned.1.call-start
  10.6 0.0 copy-done.2
  10.6 0.1 constant_dynamic-slice_fusion.1
  10.7 0.1 eq.8
  10.8 46.5 %all-gather.3.cloned.1.call-done = bf16[24,256,256]{2,1,0:T(8,128)(2,1)} async-done(((bf16[6,256,256]{2,1,0:T(8,128)(2,1)}), bf16[24,256,256]{2,1,0:T(8,128)(2,1)}) %all-gather.3.cloned.1.call-update) | async-done | bytes 3145744 | tf_op jit(solution)/shard_map/all_gather | solution.py:25
  57.3 3.7 %copy.16 = bf16[3,8,256,256]{3,1,2,0:T(8,128)(2,1)S(1)} copy(bf16[3,8,256,256]{3,2,1,0:T(8,128)(2,1)} %bitcast.40) | data formatting | bytes 6291456
  60.9 1.0 convolution_convert_fusion.1
  62.0 0.7 copy.17
  62.7 1.7 slice.11
  64.4 0.0 copy-done
  64.4 0.0 copy-start.1
  64.4 5.0 %and_select_fusion.2 = f32[6,256,256]{2,1,0:T(8,128)} fusion(bf16[3,6,256,256]{3,2,1,0:T(8,128)(2,1)S(1)} %copy-done, bf16[3,6,256,256]{3,2,1,0:T(8,128)(2,1)} %bitcast.43, bf16[3,6,256,256]{3,2,1,0:T(8,128)(2,1)} %param.6, pred[6,256]{1,0:T(8,128)(4,1)S(1)} %get-tuple-element.8, pred[6,256]{1,0:T(8,128)(4,1)S(1)} %get-tuple-element.9), kind=kOutput, calls=%fused_computation.4 | convolution fusion | flops 1209925632 | bytes 8653824 | tf_op jit(solution)/shard_map/bkil,bkml->bkim/dot_general | solution.py:41
  69.4 0.0 all-reduce.3.cloned.1.call-update
  69.4 0.0 all-gather.5.cloned.1.call-start
  69.5 62.0 %all-reduce.3.cloned.1.call-done = f32[6,256,256]{2,1,0:T(8,128)} async-done(((f32[6,256,256]{2,1,0:T(8,128)}), f32[6,256,256]{2,1,0:T(8,128)}) %all-reduce.3.cloned.1.call-update) | async-done | bytes 1572880 | tf_op jit(solution)/shard_map/psum | solution.py:57
  131.5 0.0 copy-done.1
  131.5 2.6 %fusion.25 = (f32[]{:T(128)}, f32[]{:T(128)}) fusion(f32[6,256,256]{2,1,0:T(8,128)} %all-reduce.3.cloned.1.call-done, bf16[6,256,256]{2,1,0:T(8,128)(2,1)S(1)} %copy-done.1, pred[6,256]{1,0:T(8,128)(4,1)S(1)} %get-tuple-element.8, pred[6,256]{1,0:T(8,128)(4,1)S(1)} %get-tuple-element.9), kind=kLoop, calls=%fused_computation.24 | loop fusion | flops 2752510 | bytes 2362376 | tf_op jit(solution)/shard_map/reduce_sum | solution.py:60
  134.1 10.4 %all-reduce = (f32[]{:T(128)}, f32[]{:T(128)}) all-reduce(f32[]{:T(128)} %get-tuple-element.3, f32[]{:T(128)} %get-tuple-element.2), channel_id=1, replica_groups=mesh['term'=8,'sector'=4] {'sector'}, use_global_device_ids=true, to_apply=%region_2.3 | all-reduce | flops 2 | bytes 16 | tf_op jit(solution)/shard_map/psum | solution.py:59
  145.9 2.6 %multiply_reduce_fusion = f32[]{:T(128)} fusion(f32[6,256,256]{2,1,0:T(8,128)} %all-reduce.3.cloned.1.call-done, f32[]{:T(128)S(6)} %div.6, bf16[6,256,256]{2,1,0:T(8,128)(2,1)S(1)} %copy-done.1, pred[6,256]{1,0:T(8,128)(4,1)S(1)} %get-tuple-element.8, pred[6,256]{1,0:T(8,128)(4,1)S(1)} %get-tuple-element.9), kind=kLoop, calls=%fused_computation.27 | loop fusion | flops 2752511 | bytes 2362376 | tf_op jit(solution)/shard_map/reduce_sum | solution.py:63
  148.5 8.6 %psum.31 = f32[]{:T(128)} all-reduce(f32[]{:T(128)} %multiply_reduce_fusion), channel_id=1, replica_groups=mesh['term'=8,'sector'=4] {'sector'}, use_global_device_ids=true, to_apply=%region_6.7 | all-reduce | flops 1 | bytes 8 | tf_op jit(solution)/shard_map/psum | solution.py:63
  157.8 2.8 %and_select_fusion.1 = bf16[6,256,256]{2,1,0:T(8,128)(2,1)} fusion(f32[6,256,256]{2,1,0:T(8,128)} %all-reduce.3.cloned.1.call-done, f32[]{:T(128)S(6)} %rsqrt.3, f32[]{:T(128)S(6)} %div.6, pred[6,256]{1,0:T(8,128)(4,1)S(1)} %get-tuple-element.8, pred[6,256]{1,0:T(8,128)(4,1)S(1)} %get-tuple-element.9, bf16[6,256,256]{2,1,0:T(8,128)(2,1)S(1)} %copy-done.1), kind=kLoop, calls=%fused_computation.3 | loop fusion | flops 3145728 | bytes 3148808 | tf_op jit(solution)/shard_map/jit(_where)/select_n | solution.py:36
  160.6 0.0 all-gather.5.cloned.1.call-update
  160.6 0.2 reduce-scatter.2.cloned.1.call-start
  160.8 42.1 %all-gather.5.cloned.1.call-done = bf16[24,256,256]{2,1,0:T(8,128)(2,1)} async-done(((bf16[6,256,256]{2,1,0:T(8,128)(2,1)}), bf16[24,256,256]{2,1,0:T(8,128)(2,1)}) %all-gather.5.cloned.1.call-update) | async-done | bytes 3145744 | tf_op jit(solution)/shard_map/all_gather | solution.py:25
  203.0 3.7 %copy.18 = bf16[3,8,256,256]{3,1,2,0:T(8,128)(2,1)S(1)} copy(bf16[3,8,256,256]{3,2,1,0:T(8,128)(2,1)} %bitcast.41) | data formatting | bytes 6291456
  206.6 1.0 convolution_convert_fusion
  207.7 0.7 copy.19
  208.4 1.7 slice.12
  210.1 4.9 %and_select_fusion = f32[6,256,256]{2,1,0:T(8,128)} fusion(bf16[3,6,256,256]{3,2,1,0:T(8,128)(2,1)S(1)} %copy-done, bf16[3,6,256,256]{3,2,1,0:T(8,128)(2,1)} %bitcast.42, bf16[3,6,256,256]{3,2,1,0:T(8,128)(2,1)} %param.6, pred[6,256]{1,0:T(8,128)(4,1)S(1)} %get-tuple-element.8, pred[6,256]{1,0:T(8,128)(4,1)S(1)} %get-tuple-element.9), kind=kOutput, calls=%fused_computation.2 | convolution fusion | flops 1209925632 | bytes 8653824 | tf_op jit(solution)/shard_map/bkil,bkml->bkim/dot_general | solution.py:41
  215.0 0.0 reduce-scatter.2.cloned.1.call-update
  215.0 1.6 constant_dynamic-slice_fusion
  216.7 32.8 %reduce-scatter.2.cloned.1.call-done = f32[6,32,256]{2,1,0:T(8,128)} async-done(((f32[6,256,256]{2,1,0:T(8,128)}), f32[6,32,256]{2,1,0:T(8,128)}) %reduce-scatter.2.cloned.1.call-update) | async-done | bytes 196624 | tf_op jit(solution)/shard_map/reduce_scatter | solution.py:66
Async XLA Ops:
  7.2 57.2 %copy-start = (bf16[3,6,256,256]{3,2,1,0:T(8,128)(2,1)S(1)}, bf16[3,6,256,256]{3,2,1,0:T(8,128)(2,1)}, u32[]{:S(2)}) copy-start(bf16[3,6,256,256]{3,2,1,0:T(8,128)(2,1)} %param.7) | copy-start | bytes 7077892
  7.2 3.4 %copy-start.2 = (s32[3,24]{1,0:T(4,128)S(1)}, s32[3,24]{1,0:T(4,128)}, u32[]{:S(2)}) copy-start(s32[3,24]{1,0:T(4,128)} %param.8) | copy-start | bytes 868
  7.2 50.1 %all-gather.3.cloned.1.call-start = ((), (), s32[]{:S(2)}) async-start(), calls=%async_computation.1 | async-start | bytes 3932160 | tf_op jit(solution)/shard_map/all_gather | solution.py:25
  10.5 120.9 %all-reduce.3.cloned.1.call-start = ((), (), s32[]{:S(2)}) async-start(), calls=%async_computation.2 | async-start | bytes 3145728 | tf_op jit(solution)/shard_map/psum | solution.py:57
  64.4 67.1 %copy-start.1 = (bf16[6,256,256]{2,1,0:T(8,128)(2,1)S(1)}, bf16[6,256,256]{2,1,0:T(8,128)(2,1)}, u32[]{:S(2)}) copy-start(bf16[6,256,256]{2,1,0:T(8,128)(2,1)} %param.5) | copy-start | bytes 2359300
  69.4 133.6 %all-gather.5.cloned.1.call-start = ((), (), s32[]{:S(2)}) async-start(), calls=%async_computation.3 | async-start | bytes 3932160 | tf_op jit(solution)/shard_map/all_gather | solution.py:25
  160.6 88.8 %reduce-scatter.2.cloned.1.call-start = ((), (), s32[]{:S(2)}) async-start(), calls=%async_computation.4 | async-start | bytes 1769472 | tf_op jit(solution)/shard_map/reduce_scatter | solution.py:66
Sparse Core Ops, SparseCore 0:
  10.7 46.5 all-gather.2
  69.5 61.8 all-reduce.2
  160.7 42.1 all-gather.4
  215.1 34.2 reduce-scatter.1
where the time goes:
time: 256 us
  waiting for transfers between devices  183 us (71%)
  blocking collectives  19 us (7%)
  between operations  15.9 us (6%)
  local copies, waits for them, and re-layouts  14.8 us (6%)
  matrix products  12 us (5%)
  other arithmetic  10.5 us (4%)
    all_gather x2, waiting for transfers between devices, fetch_blocks(): pieces = lax.all_gather(masked, 'sector', axis=0, tiled=True)  88.6 us
    psum x1, waiting for transfers between devices, body(): whole_sum = lax.psum(partial_value, 'term')  62 us
    reduce_scatter x1, waiting for transfers between devices, body(): lax.psum_scatter(second_partial, 'term', scatter_dimension=1, tiled=True)  32.8 us
    unnamed x12, local copies, waits for them, and re-layouts  12.1 us
    psum x1, blocking collectives, body(): lax.psum((jnp.sum(masked_float * whole_sum), jnp.sum(masked_float * maske...  10.4 us
    dot_general x2, matrix products, apply_operator(): jnp.einsum('bkil,bkml->bkim', half_product, right_env, preferred_element_...  9.96 us
    psum x1, blocking collectives, body(): spread = lax.psum(jnp.sum(residual * residual), 'sector')  8.58 us
    select_n x2, other arithmetic, apply_operator(): masked = jnp.where(keep, vector, jnp.zeros_like(vector))  5.17 us
  transfers between devices with their start and end apart: 4, of which 4 were waited for; matrix products, arithmetic and copies ran while one was open for 1% of the time, Pallas kernels for 0%

commit v1 on v0

--- a/solution.py
+++ b/solution.py
@@ -22,7 +22,9 @@
     wanted = lax.dynamic_slice_in_dim(source, my_index * local_count, local_count, 1).reshape(
         item_count
     )
-    pieces = lax.all_gather(masked, "sector", axis=0, tiled=True)
+    pieces = jnp.concatenate(
+        lax.all_to_all(jnp.stack([masked] * lax.axis_size("sector")), "sector", 0, 0), axis=0
+    )
     piece_count = pieces.shape[0]
     numbers = jnp.arange(piece_count, dtype=jnp.int32)
     onehot = (wanted[:, None] == numbers[None, :]).astype(jnp.bfloat16)

time: 256 us -> 241 us (0.941)
  waiting for transfers between devices: 183 us -> 130 us
  blocking collectives: 19 us -> 52.9 us
  starting transfers between devices: 0.34 us -> 5.37 us
    all_gather x2 -> x0, waiting for transfers between devices: 88.6 us -> none  [fetch_blocks(): pieces = lax.all_gather(masked, 'sector', axis=0, tiled=True)]
    all_to_all x0 -> x1, waiting for transfers between devices: none -> 37 us  [fetch_blocks(): lax.all_to_all(jnp.stack([masked] * lax.axis_size('sector')), 'sector', 0...]
    all_to_all x0 -> x1, blocking collectives: none -> 33.9 us  [fetch_blocks(): lax.all_to_all(jnp.stack([masked] * lax.axis_size('sector')), 'sector', 0...]
    all_to_all x0 -> x1, starting transfers between devices: none -> 5.32 us  [fetch_blocks(): lax.all_to_all(jnp.stack([masked] * lax.axis_size('sector')), 'sector', 0...]
  transfers between devices with their start and end apart: 4 -> 3, of which waited for: 4 -> 3; matrix products, arithmetic and copies ran while one was open for 1% -> 1% of each run, Pallas kernels for 0% -> 0%
where the time goes in v1:
time: 241 us
  waiting for transfers between devices  130 us (54%)
  blocking collectives  52.9 us (22%)
  between operations  16.1 us (7%)
  local copies, waits for them, and re-layouts  15.2 us (6%)
  matrix products  12 us (5%)
  other arithmetic  8.73 us (4%)
  starting transfers between devices  5.37 us (2%)
    psum x1, waiting for transfers between devices, body(): whole_sum = lax.psum(partial_value, 'term')  62.5 us
    all_to_all x1, waiting for transfers between devices, fetch_blocks(): lax.all_to_all(jnp.stack([masked] * lax.axis_size('sector')), 'sector', 0...  37 us
    all_to_all x1, blocking collectives, fetch_blocks(): lax.all_to_all(jnp.stack([masked] * lax.axis_size('sector')), 'sector', 0...  33.9 us
    reduce_scatter x1, waiting for transfers between devices, body(): lax.psum_scatter(second_partial, 'term', scatter_dimension=1, tiled=True)  30.8 us
    psum x1, blocking collectives, body(): lax.psum((jnp.sum(masked_float * whole_sum), jnp.sum(masked_float * maske...  10.4 us
    unnamed x12, local copies, waits for them, and re-layouts  10.2 us
    dot_general x2, matrix products, apply_operator(): jnp.einsum('bkil,bkml->bkim', half_product, right_env, preferred_element_...  9.98 us
    psum x1, blocking collectives, body(): spread = lax.psum(jnp.sum(residual * residual), 'sector')  8.58 us
  transfers between devices with their start and end apart: 3, of which 3 were waited for; matrix products, arithmetic and copies ran while one was open for 1% of the time, Pallas kernels for 0%

profile of v1, /device:TPU:0, one launch (start us, length us, event | category | flops | bytes accessed | tf_op | source)
XLA Modules:
  0.0 240.6 jit_solution(7244490416886828420)
XLA Ops:
  7.2 0.0 copy-start
  7.2 0.8 slice_bitcast_fusion.1
  8.0 0.1 iota_compare_fusion.3
  8.1 1.5 and_select_fusion.3
  9.6 2.0 stack.4
  11.6 0.0 copy-start.2
  11.6 5.3 %all-to-all-start = ((bf16[4,6,256,256]{3,2,1,0:T(8,128)(2,1)}), bf16[4,6,256,256]{3,2,1,0:T(8,128)(2,1)}, u32[]{:S(2)}, u32[]{:S(2)}) async-start(bf16[4,6,256,256]{3,2,1,0:T(8,128)(2,1)} %stack.4), calls=%async_computation | async-start | bytes 6291456 | tf_op jit(solution)/shard_map/all_to_all | solution.py:26
  16.9 0.0 all-reduce.3.cloned.1.call-start
  17.0 0.0 copy-done.2
  17.0 0.1 constant_dynamic-slice_fusion.1
  17.0 0.1 eq.8
  17.1 37.0 %all-to-all-done = bf16[4,6,256,256]{3,2,1,0:T(8,128)(2,1)} async-done(((bf16[4,6,256,256]{3,2,1,0:T(8,128)(2,1)}), bf16[4,6,256,256]{3,2,1,0:T(8,128)(2,1)}, u32[]{:S(2)}, u32[]{:S(2)}) %all-to-all-start) | async-done | bytes 3145760 | tf_op jit(solution)/shard_map/all_to_all | solution.py:26
  54.1 3.7 %copy.14 = bf16[3,8,256,256]{3,1,2,0:T(8,128)(2,1)S(1)} copy(bf16[3,8,256,256]{3,2,1,0:T(8,128)(2,1)} %bitcast.9) | data formatting | bytes 6291456
  57.8 1.0 convolution_convert_fusion.1
  58.8 0.7 copy.15
  59.5 1.6 slice.11
  61.2 0.0 copy-done
  61.2 0.0 copy-start.1
  61.2 5.0 %and_select_fusion.2 = f32[6,256,256]{2,1,0:T(8,128)} fusion(bf16[3,6,256,256]{3,2,1,0:T(8,128)(2,1)S(1)} %copy-done, bf16[3,6,256,256]{3,2,1,0:T(8,128)(2,1)} %bitcast.44, bf16[3,6,256,256]{3,2,1,0:T(8,128)(2,1)} %param.6, pred[6,256]{1,0:T(8,128)(4,1)S(1)} %get-tuple-element.8, pred[6,256]{1,0:T(8,128)(4,1)S(1)} %get-tuple-element.9), kind=kOutput, calls=%fused_computation.4 | convolution fusion | flops 1209925632 | bytes 8653824 | tf_op jit(solution)/shard_map/bkil,bkml->bkim/dot_general | solution.py:43
  66.2 0.0 all-reduce.3.cloned.1.call-update
  66.2 0.0 reduce-scatter.2.cloned.1.call-start
  66.3 62.5 %all-reduce.3.cloned.1.call-done = f32[6,256,256]{2,1,0:T(8,128)} async-done(((f32[6,256,256]{2,1,0:T(8,128)}), f32[6,256,256]{2,1,0:T(8,128)}) %all-reduce.3.cloned.1.call-update) | async-done | bytes 1572880 | tf_op jit(solution)/shard_map/psum | solution.py:59
  128.8 0.0 copy-done.1
  128.8 2.6 %fusion.25 = (f32[]{:T(128)}, f32[]{:T(128)}) fusion(f32[6,256,256]{2,1,0:T(8,128)} %all-reduce.3.cloned.1.call-done, bf16[6,256,256]{2,1,0:T(8,128)(2,1)S(1)} %copy-done.1, pred[6,256]{1,0:T(8,128)(4,1)S(1)} %get-tuple-element.8, pred[6,256]{1,0:T(8,128)(4,1)S(1)} %get-tuple-element.9), kind=kLoop, calls=%fused_computation.24 | loop fusion | flops 2752510 | bytes 2362376 | tf_op jit(solution)/shard_map/reduce_sum | solution.py:62
  131.4 10.4 %all-reduce = (f32[]{:T(128)}, f32[]{:T(128)}) all-reduce(f32[]{:T(128)} %get-tuple-element.3, f32[]{:T(128)} %get-tuple-element.2), channel_id=1, replica_groups=mesh['term'=8,'sector'=4] {'sector'}, use_global_device_ids=true, to_apply=%region_2.3 | all-reduce | flops 2 | bytes 16 | tf_op jit(solution)/shard_map/psum | solution.py:61
  143.2 2.6 %multiply_reduce_fusion = f32[]{:T(128)} fusion(f32[6,256,256]{2,1,0:T(8,128)} %all-reduce.3.cloned.1.call-done, f32[]{:T(128)S(6)} %div.6, bf16[6,256,256]{2,1,0:T(8,128)(2,1)S(1)} %copy-done.1, pred[6,256]{1,0:T(8,128)(4,1)S(1)} %get-tuple-element.8, pred[6,256]{1,0:T(8,128)(4,1)S(1)} %get-tuple-element.9), kind=kLoop, calls=%fused_computation.27 | loop fusion | flops 2752511 | bytes 2362376 | tf_op jit(solution)/shard_map/reduce_sum | solution.py:65
  145.8 8.6 %psum.31 = f32[]{:T(128)} all-reduce(f32[]{:T(128)} %multiply_reduce_fusion), channel_id=1, replica_groups=mesh['term'=8,'sector'=4] {'sector'}, use_global_device_ids=true, to_apply=%region_6.7 | all-reduce | flops 1 | bytes 8 | tf_op jit(solution)/shard_map/psum | solution.py:65
  155.1 1.9 and_select_fusion.1
  157.1 0.3 stack.5
  157.4 33.9 %all_to_all.10 = bf16[4,6,256,256]{3,2,1,0:T(8,128)(2,1)S(1)} all-to-all(bf16[4,6,256,256]{3,2,1,0:T(8,128)(2,1)S(1)} %stack.5), channel_id=1, replica_groups=mesh['term'=8,'sector'=4] {'sector'}, dimensions={0} | all-to-all | bytes 6291456 | tf_op jit(solution)/shard_map/all_to_all | solution.py:26
  191.3 1.8 copy.16
  193.0 1.0 convolution_convert_fusion
  194.1 0.7 copy.17
  194.8 1.6 slice.12
  196.4 5.0 %and_select_fusion = f32[6,256,256]{2,1,0:T(8,128)} fusion(bf16[3,6,256,256]{3,2,1,0:T(8,128)(2,1)S(1)} %copy-done, bf16[3,6,256,256]{3,2,1,0:T(8,128)(2,1)} %bitcast.43, bf16[3,6,256,256]{3,2,1,0:T(8,128)(2,1)} %param.6, pred[6,256]{1,0:T(8,128)(4,1)S(1)} %get-tuple-element.8, pred[6,256]{1,0:T(8,128)(4,1)S(1)} %get-tuple-element.9), kind=kOutput, calls=%fused_computation.2 | convolution fusion | flops 1209925632 | bytes 8653824 | tf_op jit(solution)/shard_map/bkil,bkml->bkim/dot_general | solution.py:43
  201.4 0.0 reduce-scatter.2.cloned.1.call-update
  201.4 1.6 constant_dynamic-slice_fusion
  203.0 30.8 %reduce-scatter.2.cloned.1.call-done = f32[6,32,256]{2,1,0:T(8,128)} async-done(((f32[6,256,256]{2,1,0:T(8,128)}), f32[6,32,256]{2,1,0:T(8,128)}) %reduce-scatter.2.cloned.1.call-update) | async-done | bytes 196624 | tf_op jit(solution)/shard_map/reduce_scatter | solution.py:68
Async XLA Ops:
  7.2 54.0 %copy-start = (bf16[3,6,256,256]{3,2,1,0:T(8,128)(2,1)S(1)}, bf16[3,6,256,256]{3,2,1,0:T(8,128)(2,1)}, u32[]{:S(2)}) copy-start(bf16[3,6,256,256]{3,2,1,0:T(8,128)(2,1)} %param.7) | copy-start | bytes 7077892
  11.6 5.3 %copy-start.2 = (s32[3,24]{1,0:T(4,128)S(1)}, s32[3,24]{1,0:T(4,128)}, u32[]{:S(2)}) copy-start(s32[3,24]{1,0:T(4,128)} %param.8) | copy-start | bytes 868
  11.6 42.5 %all-to-all-start = ((bf16[4,6,256,256]{3,2,1,0:T(8,128)(2,1)}), bf16[4,6,256,256]{3,2,1,0:T(8,128)(2,1)}, u32[]{:S(2)}, u32[]{:S(2)}) async-start(bf16[4,6,256,256]{3,2,1,0:T(8,128)(2,1)} %stack.4), calls=%async_computation | async-start | bytes 6291456 | tf_op jit(solution)/shard_map/all_to_all | solution.py:26
  16.9 111.9 %all-reduce.3.cloned.1.call-start = ((), (), s32[]{:S(2)}) async-start(), calls=%async_computation.3 | async-start | bytes 3145728 | tf_op jit(solution)/shard_map/psum | solution.py:59
  61.2 67.6 %copy-start.1 = (bf16[6,256,256]{2,1,0:T(8,128)(2,1)S(1)}, bf16[6,256,256]{2,1,0:T(8,128)(2,1)}, u32[]{:S(2)}) copy-start(bf16[6,256,256]{2,1,0:T(8,128)(2,1)} %param.5) | copy-start | bytes 2359300
  66.2 167.6 %reduce-scatter.2.cloned.1.call-start = ((), (), s32[]{:S(2)}) async-start(), calls=%async_computation.4 | async-start | bytes 1769472 | tf_op jit(solution)/shard_map/reduce_scatter | solution.py:68
Sparse Core Ops, SparseCore 0:
  66.3 62.4 all-reduce.2
  201.5 32.2 reduce-scatter.1
